TPU v7x, 128 devices: a whole 4x4x4 slice. The times are simulated.
128 devices in a mesh: aa: 16 (over x, z), ba: 8 (over y, core).
Axes of the slice: x: 4, y: 4, z: 4, core: 2. Of those that a mesh axis runs over, the one named last changes fastest.
Arguments:
- grid_features: bfloat16 [128, 128, 256, 128], P('aa', 'ba'), may hold values from -6 to 6
- weight_real: bfloat16 [32, 32, 16, 128, 128], P('ba', None, 'aa'), may hold values from -6 to 6
- weight_imag: bfloat16 [32, 32, 16, 128, 128], P('ba', None, 'aa'), may hold values from -6 to 6
- mode_keep: int32 [32, 16], P('ba', 'aa'), may hold values from 1 to 16, as said below
- local_weight: bfloat16 [128, 128], replicated, may hold values from -0.5 to 0.5
- local_bias: bfloat16 [128], replicated, may hold values from -3 to 3
Outputs:
- layer_output: bfloat16 [128, 128, 256, 128], P('aa', 'ba')
Inputs may be any that keep to these rules, and one draw needn't show every extreme that they name: mode_keep[i, k] counts the retained levels of the second frequency on the line of the i-th retained first frequency and the k-th third frequency.
All inputs are finite; a program needn't handle non-finite values.
Results may differ from a plain program's by a relative error of at most 0.012.
Values may be sent and summed in bfloat16 or wider, within the bound.
A program may use at most 128 MiB of HBM per device.

v0:
```python
import math

import jax
import jax.numpy as jnp
from jax import lax
from jax.sharding import PartitionSpec as P

NX = 128
NY = 128
NZ = 256
KX = 32
KY = 32
KZ = 16


def sent_together(arrays, axis, split_dim, concat_dim, along):
    both = jnp.concatenate(arrays, axis=along)
    whole, at, done = (
        lax.all_to_all(both, axis, split_axis=split_dim, concat_axis=concat_dim, tiled=True),
        0,
        [],
    )
    for a in arrays:
        done.append(lax.slice_in_dim(whole, at, at + a.shape[along], axis=along))
        at += a.shape[along]
    return tuple(done)


def kept_modes(length, number):
    positions = jnp.arange(number, dtype=jnp.int32)
    return jnp.where(positions < number // 2, positions, positions + (length - number))


def phase_tables(length, mode_list):
    places = jnp.arange(length, dtype=jnp.int32)
    phase_steps = places[:, None] * mode_list[None, :] % length
    angles = phase_steps.astype(jnp.float32) * (2.0 * math.pi / length)
    return (jnp.cos(angles), jnp.sin(angles))


def forward_kernel(length, number):
    cosine_table, sine_table = phase_tables(length, kept_modes(length, number))
    upper_rows = jnp.concatenate([cosine_table, -sine_table], axis=1)
    lower_rows = jnp.concatenate([sine_table, cosine_table], axis=1)
    return jnp.concatenate([upper_rows, lower_rows], axis=0)


def inverse_kernel(length, number):
    cosine_table, sine_table = phase_tables(length, kept_modes(length, number))
    upper_rows = jnp.concatenate([cosine_table.T, sine_table.T], axis=1)
    lower_rows = jnp.concatenate([-sine_table.T, cosine_table.T], axis=1)
    return jnp.concatenate([upper_rows, lower_rows], axis=0)


def depth_kernels():
    cosine_table, sine_table = phase_tables(NZ, jnp.arange(KZ, dtype=jnp.int32))
    forward = jnp.concatenate([cosine_table, -sine_table], axis=1).astype(jnp.bfloat16)
    factor = jnp.where(jnp.arange(KZ, dtype=jnp.int32) == 0, 1.0, 2.0).astype(jnp.float32) / (
        NX * NY * NZ
    )
    inverse = jnp.concatenate(
        [cosine_table.T * factor[:, None], -sine_table.T * factor[:, None]], axis=0
    ).astype(jnp.bfloat16)
    return (forward, inverse)


def along_first(operand, kernel):
    return jnp.einsum("pabc,pq->qabc", operand, kernel, preferred_element_type=jnp.float32)


def along_second(operand, kernel):
    return jnp.einsum("apbc,pq->aqbc", operand, kernel, preferred_element_type=jnp.float32)


def mode_mask(kept_counts):
    positions = jnp.arange(KY, dtype=jnp.int32)
    levels = jnp.where(positions < KY // 2, positions, KY - 1 - positions)
    return (levels[None, :, None] < kept_counts[:, None, :]).astype(jnp.float32)


def mix_modes(spec_real, spec_imag, weight_real, weight_imag, kept_counts):
    pattern = "abcd,abcde->abce"
    out_real = jnp.einsum(
        pattern, spec_real, weight_real, preferred_element_type=jnp.float32
    ) - jnp.einsum(pattern, spec_imag, weight_imag, preferred_element_type=jnp.float32)
    out_imag = jnp.einsum(
        pattern, spec_real, weight_imag, preferred_element_type=jnp.float32
    ) + jnp.einsum(pattern, spec_imag, weight_real, preferred_element_type=jnp.float32)
    keep_mask = mode_mask(kept_counts)[..., None]
    return (out_real * keep_mask, out_imag * keep_mask)


def per_device(grid_features, weight_real, weight_imag, mode_keep, local_weight, local_bias):
    forward_depth, inverse_depth = depth_kernels()
    coeffs = jnp.einsum(
        "xyzc,zk->xykc", grid_features, forward_depth, preferred_element_type=jnp.float32
    ).astype(jnp.bfloat16)
    depth_real = coeffs[:, :, :KZ]
    depth_imag = coeffs[:, :, KZ:]
    gathered = sent_together((depth_real, depth_imag), "aa", 2, 0, 1)
    result = along_first(
        jnp.concatenate(gathered, axis=0).astype(jnp.float32), forward_kernel(NX, KX)
    )
    gathered = tuple(
        (
            part.astype(jnp.float32)
            for part in sent_together(
                (result[:KX].astype(jnp.bfloat16), result[KX:].astype(jnp.bfloat16)), "ba", 0, 1, 2
            )
        )
    )
    result = along_second(jnp.concatenate(gathered, axis=1), forward_kernel(NY, KY)).astype(
        jnp.bfloat16
    )
    mixed_real, mixed_imag = mix_modes(
        result[:, :KY], result[:, KY:], weight_real, weight_imag, mode_keep
    )
    result = along_second(jnp.concatenate([mixed_real, mixed_imag], axis=1), inverse_kernel(NY, KY))
    gathered = tuple(
        (
            part.astype(jnp.float32)
            for part in sent_together(
                (result[:, :NY].astype(jnp.bfloat16), result[:, NY:].astype(jnp.bfloat16)),
                "ba",
                1,
                0,
                2,
            )
        )
    )
    result = along_first(jnp.concatenate(gathered, axis=0), inverse_kernel(NX, KX)).astype(
        jnp.bfloat16
    )
    back_field = sent_together((result[:NX], result[NX:]), "aa", 0, 2, 1)
    spectral = jnp.einsum(
        "xykc,kz->xyzc",
        jnp.concatenate(back_field, axis=2),
        inverse_depth,
        preferred_element_type=jnp.float32,
    )
    local_term = jnp.einsum(
        "xyzc,cd->xyzd", grid_features, local_weight, preferred_element_type=jnp.float32
    )
    return jax.nn.gelu(spectral + local_term + local_bias.astype(jnp.float32)).astype(jnp.bfloat16)


def solution(mesh):
    in_specs = (
        P("aa", "ba", None, None),
        P("ba", None, "aa", None, None),
        P("ba", None, "aa", None, None),
        P("ba", "aa"),
        P(),
        P(),
    )
    out_specs = P("aa", "ba", None, None)
    return jax.shard_map(
        per_device, mesh=mesh, in_specs=in_specs, out_specs=out_specs, check_vma=False
    )
```

profile of v0, /device:TPU:0, one launch (start us, length us, event | category | flops | bytes accessed | tf_op | source)
XLA Modules:
  0.0 111.0 jit_solution(3319638627525551025)
XLA Ops:
  0.0 0.0 copy-start
  0.0 0.1 negate_convert_fusion
  0.1 4.9 %fusion.17 = bf16[8,16,32,128]{3,2,1,0:T(8,128)(2,1)S(1)} fusion(bf16[8,16,256,128]{3,2,1,0:T(8,128)(2,1)} %param.6, bf16[256,16]{0,1:T(8,128)(2,1)S(1)} %get-tuple-element.33, bf16[256,16]{0,1:T(8,128)(2,1)S(1)} %get-tuple-element.34), kind=kOutput, calls=%fused_computation.21 | convolution fusion | flops 268992512 | bytes 9453568 | tf_op jit(solution)/shard_map/xyzc,zk->xykc/dot_general | solution.py:95
  5.0 0.0 copy-start.3
  5.0 0.3 fusion.83
  5.3 0.1 pad_maximum_fusion
  5.4 1.2 %copy.24 = bf16[8,32,16,128]{3,1,0,2:T(8,128)(2,1)} copy(bf16[8,32,16,128]{3,2,1,0:T(8,128)(2,1)S(1)} %pad_maximum_fusion) | data formatting | bytes 2097152 | tf_op jit(solution)/shard_map/concatenate | solution.py:17
  6.7 8.0 %all-to-all-start = ((bf16[8,32,16,128]{3,1,0,2:T(8,128)(2,1)}), bf16[8,32,16,128]{3,1,0,2:T(8,128)(2,1)S(1)}, u32[]{:S(2)}, u32[]{:S(2)}) async-start(bf16[8,32,16,128]{3,1,0,2:T(8,128)(2,1)} %copy.24), calls=%async_computation | async-start | bytes 2097152 | tf_op jit(solution)/shard_map/all_to_all | solution.py:19
  14.7 0.2 fusion.70
  14.8 17.6 %all-to-all-done = bf16[8,32,16,128]{3,1,0,2:T(8,128)(2,1)S(1)} async-done(((bf16[8,32,16,128]{3,1,0,2:T(8,128)(2,1)}), bf16[8,32,16,128]{3,1,0,2:T(8,128)(2,1)S(1)}, u32[]{:S(2)}, u32[]{:S(2)}) %all-to-all-start) | async-done | bytes 1048608 | tf_op jit(solution)/shard_map/all_to_all | solution.py:19
  32.4 0.2 fusion.82
  32.6 0.1 copy.42
  32.7 0.1 copy.43
  32.9 0.3 convolution_convert_fusion.3
  33.2 0.8 copy.27
  34.0 4.5 %all-to-all-start.1 = ((bf16[32,16,2,128]{3,1,2,0:T(8,128)(2,1)}), bf16[32,16,2,128]{3,1,2,0:T(8,128)(2,1)S(1)}, u32[]{:S(2)}, u32[]{:S(2)}) async-start(bf16[32,16,2,128]{3,1,2,0:T(8,128)(2,1)} %copy.27), calls=%async_computation.1 | async-start | bytes 524288 | tf_op jit(solution)/shard_map/all_to_all | solution.py:19
  38.5 0.0 copy-done.3
  38.5 0.1 compare_convert_fusion
  38.6 0.2 fusion.67
  38.8 7.3 %all-to-all-done.1 = bf16[32,16,2,128]{3,1,2,0:T(8,128)(2,1)S(1)} async-done(((bf16[32,16,2,128]{3,1,2,0:T(8,128)(2,1)}), bf16[32,16,2,128]{3,1,2,0:T(8,128)(2,1)S(1)}, u32[]{:S(2)}, u32[]{:S(2)}) %all-to-all-start.1) | async-done | bytes 262176 | tf_op jit(solution)/shard_map/all_to_all | solution.py:19
  46.1 0.2 fusion.19
  46.3 0.0 copy-start.2
  46.3 3.5 %fusion.13 = f32[4,32,1,128]{3,2,1,0:T(1,128)S(1)} fusion(bf16[4,32,1,128,128]{4,3,2,1,0:T(8,128)(2,1)} %param.7, bf16[4,32,128,1]{2,1,0,3:T(8,128)(2,1)S(1)} %get-tuple-element.21), kind=kOutput, calls=%fused_computation.15 | convolution fusion | flops 4194304 | bytes 4292608 | tf_op jit(solution)/shard_map/abcd,abcde->abce/dot_general | solution.py:88
  49.8 3.4 %fusion.11 = f32[4,32,1,128]{3,2,1,0:T(1,128)S(1)} fusion(bf16[4,32,1,128,128]{4,3,2,1,0:T(8,128)(2,1)} %param.8, bf16[4,32,128,1]{2,1,0,3:T(8,128)(2,1)S(1)} %get-tuple-element.21), kind=kOutput, calls=%fused_computation.13 | convolution fusion | flops 4194304 | bytes 4292608 | tf_op jit(solution)/shard_map/abcd,abcde->abce/dot_general | solution.py:85
  53.2 0.0 copy-done.1
  53.2 1.2 %fusion.9 = f32[4,32,1,128]{3,2,1,0:T(1,128)S(1)} fusion(bf16[4,32,1,128,128]{4,3,2,1,0:T(8,128)(2,1)S(1)} %copy-done.1, bf16[4,32,128,1]{2,1,0,3:T(8,128)(2,1)S(1)} %get-tuple-element.22), kind=kOutput, calls=%fused_computation.11 | convolution fusion | flops 4194304 | bytes 4292608 | tf_op jit(solution)/shard_map/abcd,abcde->abce/dot_general | solution.py:86
  54.4 0.0 copy-done.2
  54.4 1.2 %fusion.15 = f32[4,32,1,128]{3,2,1,0:T(1,128)S(1)} fusion(bf16[4,32,1,128,128]{4,3,2,1,0:T(8,128)(2,1)S(1)} %copy-done.2, bf16[4,32,128,1]{2,1,0,3:T(8,128)(2,1)S(1)} %get-tuple-element.22), kind=kOutput, calls=%fused_computation.17 | convolution fusion | flops 4194304 | bytes 4292608 | tf_op jit(solution)/shard_map/abcd,abcde->abce/dot_general | solution.py:83
  55.6 0.1 multiply_bitcast_fusion.1
  55.7 0.2 fusion.18
  56.0 0.2 copy.29
  56.2 9.9 %all_to_all.72 = bf16[4,128,2,128]{3,0,2,1:T(4,128)(2,1)S(1)} all-to-all(bf16[4,128,2,128]{3,0,2,1:T(4,128)(2,1)S(1)} %copy.29), channel_id=1, replica_groups=mesh['aa'=16,'ba'=8] {'ba'}, dimensions={1} | all-to-all | bytes 524288 | tf_op jit(solution)/shard_map/all_to_all | solution.py:19
  66.1 0.1 copy.30
  66.3 0.5 convolution_convert_fusion
  66.7 0.1 slice_bitcast_fusion.1
  66.8 0.1 pad_maximum_fusion.1
  66.9 1.6 %copy.31 = bf16[128,32,1,128]{3,1,2,0:T(8,128)(2,1)} copy(bf16[128,32,1,128]{3,0,1,2:T(8,128)(2,1)S(1)} %pad_maximum_fusion.1) | data formatting | bytes 2097152 | tf_op jit(solution)/shard_map/concatenate | solution.py:17
  68.5 3.8 %all-to-all-start.3 = ((bf16[128,32,1,128]{3,1,2,0:T(8,128)(2,1)}), bf16[128,32,1,128]{3,1,2,0:T(8,128)(2,1)S(1)}, u32[]{:S(2)}, u32[]{:S(2)}) async-start(bf16[128,32,1,128]{3,1,2,0:T(8,128)(2,1)} %copy.31), calls=%async_computation.3 | async-start | bytes 2097152 | tf_op jit(solution)/shard_map/all_to_all | solution.py:19
  72.4 0.1 multiply_convert_fusion.1
  72.5 17.3 %all-to-all-done.3 = bf16[128,32,1,128]{3,1,2,0:T(8,128)(2,1)S(1)} async-done(((bf16[128,32,1,128]{3,1,2,0:T(8,128)(2,1)}), bf16[128,32,1,128]{3,1,2,0:T(8,128)(2,1)S(1)}, u32[]{:S(2)}, u32[]{:S(2)}) %all-to-all-start.3) | async-done | bytes 1048608 | tf_op jit(solution)/shard_map/all_to_all | solution.py:19
  89.8 0.7 copy.53
  90.5 0.0 slice-start
  90.5 0.2 fusion.81
  90.7 0.0 slice-start.1
  90.7 8.1 %fusion.22 = f32[256,8,16,128]{3,0,2,1:T(8,128)} fusion(bf16[8,16,16,128]{3,2,1,0:T(8,128)(2,1)S(1)} %get-tuple-element.6, bf16[8,16,16,128]{3,2,1,0:T(8,128)(2,1)S(1)} %get-tuple-element.5, bf16[16,256]{1,0:T(8,128)(2,1)S(1)} %get-tuple-element.26, bf16[16,256]{1,0:T(8,128)(2,1)S(1)} %get-tuple-element.25), kind=kOutput, calls=%fused_computation.32 | convolution fusion | flops 270565376 | bytes 17842176 | tf_op jit(solution)/shard_map/xykc,kz->xyzc/dot_general | solution.py:135
  98.8 0.0 copy-done
  98.8 0.0 slice-done.1
  98.8 12.2 %fusion.7 = bf16[8,16,256,128]{3,2,1,0:T(8,128)(2,1)} fusion(f32[256,8,16,128]{3,0,2,1:T(8,128)} %fusion.22, bf16[8,16,256,128]{3,2,1,0:T(8,128)(2,1)S(1)} %bitcast.110, f32[128]{0:T(128)S(1)} %convert_element_type.97, bf16[128,128]{1,0:T(8,128)(2,1)S(1)} %copy-done), kind=kOutput, calls=%fused_computation.8 | convolution fusion | flops 1119879168 | bytes 33587712 | tf_op jit(solution)/shard_map/xyzc,cd->xyzd/dot_general | solution.py:141
  (17 shorter events, 0.2 us)
Async XLA Ops:
  0.0 98.8 %copy-start = (bf16[128,128]{1,0:T(8,128)(2,1)S(1)}, bf16[128,128]{1,0:T(8,128)(2,1)}, u32[]{:S(2)}) copy-start(bf16[128,128]{1,0:T(8,128)(2,1)} %param.10) | copy-start | bytes 98308
  5.0 33.5 %copy-start.3 = (s32[4,1]{0,1:T(1,128)S(1)}, s32[4,1]{0,1:T(1,128)}, u32[]{:S(2)}) copy-start(s32[4,1]{0,1:T(1,128)} %param.9) | copy-start | bytes 52
  6.7 25.7 %all-to-all-start = ((bf16[8,32,16,128]{3,1,0,2:T(8,128)(2,1)}), bf16[8,32,16,128]{3,1,0,2:T(8,128)(2,1)S(1)}, u32[]{:S(2)}, u32[]{:S(2)}) async-start(bf16[8,32,16,128]{3,1,0,2:T(8,128)(2,1)} %copy.24), calls=%async_computation | async-start | bytes 2097152 | tf_op jit(solution)/shard_map/all_to_all | solution.py:19
  34.0 12.0 %all-to-all-start.1 = ((bf16[32,16,2,128]{3,1,2,0:T(8,128)(2,1)}), bf16[32,16,2,128]{3,1,2,0:T(8,128)(2,1)S(1)}, u32[]{:S(2)}, u32[]{:S(2)}) async-start(bf16[32,16,2,128]{3,1,2,0:T(8,128)(2,1)} %copy.27), calls=%async_computation.1 | async-start | bytes 524288 | tf_op jit(solution)/shard_map/all_to_all | solution.py:19
  46.0 7.2 %copy-start.1 = (bf16[4,32,1,128,128]{4,3,2,1,0:T(8,128)(2,1)S(1)}, bf16[4,32,1,128,128]{4,3,2,1,0:T(8,128)(2,1)}, u32[]{:S(2)}) copy-start(bf16[4,32,1,128,128]{4,3,2,1,0:T(8,128)(2,1)} %param.8) | copy-start | bytes 12582916
  46.3 8.1 %copy-start.2 = (bf16[4,32,1,128,128]{4,3,2,1,0:T(8,128)(2,1)S(1)}, bf16[4,32,1,128,128]{4,3,2,1,0:T(8,128)(2,1)}, u32[]{:S(2)}) copy-start(bf16[4,32,1,128,128]{4,3,2,1,0:T(8,128)(2,1)} %param.7) | copy-start | bytes 12582916
  55.6 16.8 %copy-start.4 = (bf16[128]{0:T(256)(128)(2,1)S(1)}, bf16[128]{0:T(256)(128)(2,1)}, u32[]{:S(2)}) copy-start(bf16[128]{0:T(256)(128)(2,1)} %param.11) | copy-start | bytes 772
  68.5 21.2 %all-to-all-start.3 = ((bf16[128,32,1,128]{3,1,2,0:T(8,128)(2,1)}), bf16[128,32,1,128]{3,1,2,0:T(8,128)(2,1)S(1)}, u32[]{:S(2)}, u32[]{:S(2)}) async-start(bf16[128,32,1,128]{3,1,2,0:T(8,128)(2,1)} %copy.31), calls=%async_computation.3 | async-start | bytes 2097152 | tf_op jit(solution)/shard_map/all_to_all | solution.py:19
  90.5 8.3 %slice-start = ((s8[8388608]{0:T(1024)(128)(4,1)}), s8[4194304]{0:T(1024)(128)(4,1)S(1)}, s32[]{:S(2)}) async-start(s8[8388608]{0:T(1024)(128)(4,1)} %bitcast.109), calls=%async_computation.4 | async-start | bytes 8388608
  90.7 8.1 %slice-start.1 = ((s8[8388608]{0:T(1024)(128)(4,1)}), s8[4194304]{0:T(1024)(128)(4,1)S(1)}, s32[]{:S(2)}) async-start(s8[8388608]{0:T(1024)(128)(4,1)} %bitcast.109), calls=%async_computation.5 | async-start | bytes 8388608
where the time goes:
time: 111 us
  waiting for transfers between devices  42.1 us (38%)
  matrix products  35.7 us (32%)
  starting transfers between devices  16.3 us (15%)
  blocking collectives  9.91 us (9%)
  local copies, waits for them, and re-layouts  5.79 us (5%)
    all_to_all x3, waiting for transfers between devices, sent_together(): lax.all_to_all(both, axis, split_axis=split_dim, concat_axis=concat_dim,...  42.1 us
    all_to_all x3, starting transfers between devices, sent_together(): lax.all_to_all(both, axis, split_axis=split_dim, concat_axis=concat_dim,...  16.3 us
    dot_general x1, matrix products, per_device(): jnp.einsum('xyzc,cd->xyzd', grid_features, local_weight, preferred_elemen...  12.2 us
    all_to_all x1, blocking collectives, sent_together(): lax.all_to_all(both, axis, split_axis=split_dim, concat_axis=concat_dim,...  9.91 us
    dot_general x1, matrix products, per_device(): jnp.einsum('xykc,kz->xyzc', jnp.concatenate(back_field, axis=2), inverse_...  8.09 us
    dot_general x1, matrix products, per_device(): jnp.einsum('xyzc,zk->xykc', grid_features, forward_depth, preferred_eleme...  4.94 us
    concatenate x4, local copies, waits for them, and re-layouts, sent_together(): both = jnp.concatenate(arrays, axis=along)  3.9 us
    dot_general x1, matrix products, mix_modes(): jnp.einsum(pattern, spec_imag, weight_real, preferred_element_type=jnp.fl...  3.52 us
  transfers between devices with their start and end apart: 3, of which 3 were waited for; matrix products, arithmetic and copies ran while one was open for 0% of the time, Pallas kernels for 0%

commit v1 on v0

v1 whole, which is shorter than its diff:
```python
import numpy as np
import jax
import jax.numpy as jnp
from jax import lax
from jax.experimental import pallas as pl
from jax.experimental.pallas import tpu as pltpu
from jax.sharding import PartitionSpec as P

NX, NY, NZ, C = 128, 128, 256, 128
KX, KY, KZ = 32, 32, 16
NA, NB = 16, 8
MESH = pl.DeviceIdType.MESH
BF = jnp.bfloat16
F32 = jnp.float32

AA_ORDER = [(1, 0), (0, 1), (3, 0), (0, 3), (2, 0), (0, 2), (1, 1), (3, 3), (1, 3), (3, 1),
            (2, 1), (2, 3), (1, 2), (3, 2), (2, 2)]
BA_ORDER = [(1, 0), (3, 0), (2, 0), (1, 1), (3, 1), (2, 1), (0, 1)]


def kept(length, number):
    j = np.arange(number)
    return np.where(j < number // 2, j, j + length - number)


def angle(k, n, length):
    return 2.0 * np.pi * ((k * n) % length) / length


def complex_block(theta, ri_out, ri_in, sign):
    c, s = np.cos(theta), sign * np.sin(theta)
    return np.where(ri_out == ri_in, c, np.where(ri_out == 0, -s, s))


def tables():
    kx, ky = kept(NX, KX), kept(NY, KY)
    k, _, r, z = np.ix_(np.arange(KZ), np.arange(4), np.arange(2), np.arange(NZ))
    th = angle(k, z, NZ)
    t1 = np.where(r == 0, np.cos(th), -np.sin(th)) + np.zeros((KZ, 4, 2, NZ))
    t1 = t1.reshape(128, 256)
    k, _, r, x, q = np.ix_(kx, np.arange(4), np.arange(2), np.arange(NX), np.arange(2))
    t2 = complex_block(angle(k, x, NX), r, q, -1) + np.zeros((KX, 4, 2, NX, 2))
    t2 = t2.reshape(256, 256)
    k, r, h, b, y, q = np.ix_(ky, np.arange(2), np.arange(2), np.arange(NB), np.arange(8), np.arange(2))
    f = complex_block(angle(k, b * 16 + h * 8 + y, NY), r, q, -1).reshape(KY, 2, 256)
    t3 = np.concatenate([f.reshape(64, 256), np.stack([-f[:, 1], f[:, 0]], axis=1).reshape(64, 256)], axis=0)
    h, b, y, m, r, n, k, q = np.ix_(np.arange(2), np.arange(NB), np.arange(8), np.arange(4), np.arange(2),
                                    np.arange(4), ky, np.arange(2))
    t4 = complex_block(angle(k, b * 16 + h * 8 + y, NY), r, q, 1) * (m == n)
    t4 = t4.reshape(1024, 256)
    y, x, r, b, w, m, q = np.ix_(np.arange(2), np.arange(NX), np.arange(2), np.arange(NB), np.arange(2),
                                 np.arange(4), np.arange(2))
    t5 = complex_block(angle(kx[b * 4 + m], x, NX), r, q, 1) * (y == w)
    t5 = t5.reshape(512, 128)
    z, k, _, r = np.ix_(np.arange(NZ), np.arange(KZ), np.arange(8), np.arange(2))
    th = angle(k, z, NZ)
    t6 = np.where(r == 0, np.cos(th), -np.sin(th)) * np.where(k == 0, 1.0, 2.0) / (NX * NY * NZ) * 0.5
    t6 = (t6 + np.zeros((NZ, KZ, 8, 2))).reshape(256, 256)
    return [np.asarray(t, np.float32).astype(jnp.bfloat16) for t in (t1, t2, t3, t4, t5, t6)]


def dot(a, b):
    return jnp.dot(a, b, preferred_element_type=F32)


def spectral_kernel(x_hbm, wr_hbm, wi_hbm, keep_ref, t1_hbm, t2_hbm, t3_hbm, t4_hbm, t5_hbm, out_ref,
                    xv, wv, t1v, t1m, t2v, t2m, t3v, t4v, t5v, s1, r1, s2, r2, s3, r3, s4,
                    xsem, wsem, tsem, sa, ra, sb, rb, sc, rc, sd, rd):
    ia, ib = lax.axis_index("aa"), lax.axis_index("ba")
    ix, iz, iy, ic = ia // 4, lax.rem(ia, 4), ib // 2, lax.rem(ib, 2)
    aa_peers = [lax.rem(ix + dx, 4) * 4 + lax.rem(iz + dz, 4) for dx, dz in AA_ORDER]
    ba_peers = [lax.rem(iy + dy, 4) * 2 + lax.rem(ic + dc, 2) for dy, dc in BA_ORDER]

    tcopies = [pltpu.make_async_copy(src, dst, tsem.at[i]) for i, (src, dst) in enumerate(
        [(t1_hbm, t1v), (t2_hbm, t2v), (t3_hbm, t3v), (t4_hbm, t4v), (t5_hbm, t5v)])]
    tcopies[0].start()
    xcopies = [pltpu.make_async_copy(x_hbm.at[:, pl.ds(4 * g, 4)], xv.at[g], xsem.at[g]) for g in range(4)]
    for c in xcopies:
        c.start()
    tcopies[1].start()
    wcopies = [pltpu.make_async_copy(wr_hbm, wv.at[0], wsem.at[0]), pltpu.make_async_copy(wi_hbm, wv.at[1], wsem.at[1])]

    barrier = pltpu.get_barrier_semaphore()
    for t in aa_peers:
        pl.semaphore_signal(barrier, inc=1, device_id={"aa": t}, device_id_type=MESH)
    for t in ba_peers:
        pl.semaphore_signal(barrier, inc=1, device_id={"ba": t}, device_id_type=MESH)

    def send_aa(src, dst, ssem, rsem):
        for t in aa_peers:
            pltpu.make_async_remote_copy(src.at[t], dst.at[ia], ssem, rsem, device_id={"aa": t}, device_id_type=MESH).start()

    def send_ba(src, dst, ssem, rsem):
        for t in ba_peers:
            pltpu.make_async_remote_copy(src(t), dst.at[ib], ssem, rsem, device_id={"ba": t}, device_id_type=MESH).start()

    def wait_bytes(ref, sem):
        pltpu.make_async_copy(ref, ref, sem).wait()

    tcopies[0].wait()
    rows1 = lax.broadcasted_iota(jnp.int32, (128, 256), 0) // 2 % 4
    for i in range(4):
        t1m[i] = jnp.where(rows1 == i, t1v[...].astype(F32), 0.0).astype(BF)
    for g in range(4):
        xcopies[g].wait()
        for y in range(4):
            acc = None
            for i in range(4):
                rhs = jnp.concatenate([xv[g, i, y], xv[g, i + 4, y]], axis=1)
                p = dot(t1m[i], rhs)
                acc = p if acc is None else acc + p
            acc = acc.reshape(KZ, 8, 256)
            s1[g, :, y] = jnp.concatenate([acc[:, :, :128], acc[:, :, 128:]], axis=1).astype(BF)
        if g == 0:
            pl.semaphore_wait(barrier, len(aa_peers) + len(ba_peers))
        send_aa(s1.at[g], r1.at[g], sa, ra.at[g])
        r1[g, ia] = s1[g, ia]

    for c in tcopies[2:] + wcopies:
        c.start()
    tcopies[1].wait()
    rows2 = lax.broadcasted_iota(jnp.int32, (256, 256), 0) // 2 % 4
    for i in range(4):
        t2m[i] = jnp.where(rows2 == i, t2v[...].astype(F32), 0.0).astype(BF)

    for h in range(2):
        for g in (2 * h, 2 * h + 1):
            wait_bytes(r1.at[g, pl.ds(0, NA - 1)], ra.at[g])
        acc = None
        for i in range(4):
            rhs = jnp.concatenate([r1[2 * h, :, i].reshape(256, C), r1[2 * h + 1, :, i].reshape(256, C)], axis=1)
            p = dot(t2m[i], rhs)
            acc = p if acc is None else acc + p
        acc = acc.reshape(KX, 8, 256)
        s2[h] = jnp.concatenate([acc[:, :, :128], acc[:, :, 128:]], axis=1).astype(BF)
        send_ba(lambda t: s2.at[h, pl.ds(4 * t, 4)], r2.at[h], sb, rb.at[h])
        r2[h, ib] = s2[h, pl.ds(4 * ib, 4)]

    for c in tcopies[2:]:
        c.wait()
    for c in wcopies:
        c.wait()
    for h in range(2):
        wait_bytes(r2.at[h, pl.ds(0, NB - 1)], rb.at[h])

    row16 = lax.broadcasted_iota(jnp.int32, (16, 256), 0) // 2 % 4
    row8 = lax.broadcasted_iota(jnp.int32, (8, C), 0) // 2
    mixed = [[], [], [], []]
    for p in range(2):
        rhs = jnp.concatenate([r2[:, :, 2 * p].reshape(256, C), r2[:, :, 2 * p + 1].reshape(256, C)], axis=1)
        spec = dot(t3v[...], rhs)
        for q in range(8):
            first, second = spec[8 * q:8 * q + 8], spec[64 + 8 * q:64 + 8 * q + 8]
            lhs = jnp.concatenate([jnp.concatenate([first[:, :C], first[:, C:]], axis=0),
                                   jnp.concatenate([second[:, :C], second[:, C:]], axis=0)], axis=1)
            acc = None
            for j in range(4):
                k = 4 * q + j
                w = jnp.concatenate([jnp.concatenate([wv[r, 2 * p, k], wv[r, 2 * p + 1, k]], axis=1) for r in range(2)], axis=0)
                part = dot(jnp.where(row16 == j, lhs, 0.0).astype(BF), w)
                acc = part if acc is None else acc + part
            position = 4 * q + row8
            level = jnp.where(position < KY // 2, position, KY - 1 - position)
            mixed[2 * p].append(jnp.where(level < keep_ref[2 * p, 0], acc[:8, :C], 0.0))
            mixed[2 * p + 1].append(jnp.where(level < keep_ref[2 * p + 1, 0], acc[8:, C:], 0.0))
    rhs = jnp.concatenate([m for line in mixed for m in line], axis=0).astype(BF)
    for h in range(2):
        s3[h] = dot(t4v[pl.ds(512 * h, 512)], rhs).astype(BF).reshape(NB, 4, 16, C)
        send_ba(lambda t: s3.at[h, t], r3.at[h], sc, rc.at[h])
        r3[h, ib] = s3[h, ib]

    for h in range(2):
        wait_bytes(r3.at[h, pl.ds(0, NB - 1)], rc.at[h])
        for g in (2 * h, 2 * h + 1):
            n = 2 * (g - 2 * h)
            rhs = jnp.concatenate([r3[h, :, n].reshape(128, C), r3[h, :, n + 1].reshape(128, C)], axis=1)
            back = dot(t5v[...], rhs).astype(BF)
            for half in range(2):
                for i in range(2):
                    s4[g, :, 2 * half + i] = back[256 * i:256 * i + 256, C * half:C * half + C].reshape(NA, 16, C)
            send_aa(s4.at[g], out_ref.at[g], sd, rd.at[g])
            out_ref[g, ia] = s4[g, ia]

    for g in range(4):
        wait_bytes(out_ref.at[g, pl.ds(0, NA - 1)], rd.at[g])
    wait_bytes(s1.at[:, pl.ds(0, NA - 1)], sa)
    wait_bytes(s4.at[:, pl.ds(0, NA - 1)], sd)
    wait_bytes(r2.at[:, pl.ds(0, NB - 1)], sb)
    wait_bytes(r3.at[:, pl.ds(0, NB - 1)], sc)


def final_kernel(x_ref, back_ref, w_ref, bias_ref, t6_ref, out_ref, t6m, wbd):
    j, xh = pl.program_id(0), pl.program_id(1)

    @pl.when((j == 0) & (xh == 0))
    def _():
        lane = lax.broadcasted_iota(jnp.int32, (256, 256), 1) // 2 % 8
        for i in range(8):
            t6m[i] = jnp.where(lane == i, t6_ref[...].astype(F32), 0.0).astype(BF)
        w = (w_ref[...].astype(F32) * 0.5).astype(BF)
        z = jnp.zeros_like(w)
        wbd[...] = jnp.concatenate([jnp.concatenate([w, z], axis=1), jnp.concatenate([z, w], axis=1)], axis=0)

    rhs = jnp.concatenate([back_ref[0, :, 0].reshape(256, C), back_ref[0, :, 1].reshape(256, C)], axis=1)
    bias = bias_ref[...].astype(F32) * 0.5
    bias = jnp.concatenate([bias, bias], axis=1)
    c0 = np.float32(2.0 * np.sqrt(2.0 / np.pi))
    c1 = np.float32(8.0 * 0.044715 * np.sqrt(2.0 / np.pi))
    for i in range(4):
        lhs = jnp.concatenate([x_ref[i, 0], x_ref[i, 1]], axis=1)
        h = dot(lhs, wbd[...]) + dot(t6m[4 * xh + i], rhs) + bias
        o = h + h * jnp.tanh(h * (c0 + c1 * (h * h)))
        o = o.astype(BF)
        out_ref[i, 0] = o[:, :C]
        out_ref[i, 1] = o[:, C:]


def per_device(grid_features, weight_real, weight_imag, mode_keep, local_weight, local_bias):
    t1, t2, t3, t4, t5, t6 = tables()
    any_spec = pl.BlockSpec(memory_space=pl.ANY)
    vmem_spec = pl.BlockSpec(memory_space=pltpu.VMEM)
    V = lambda *s: pltpu.VMEM(s, BF)
    D = pltpu.SemaphoreType.DMA
    back = pl.pallas_call(
        spectral_kernel,
        out_shape=jax.ShapeDtypeStruct((4, NA, 4, 16, C), BF),
        in_specs=[any_spec] * 3 + [pl.BlockSpec(memory_space=pltpu.SMEM)] + [any_spec] * 5,
        out_specs=vmem_spec,
        scratch_shapes=[
            V(4, 8, 4, NZ, C), V(2, 4, KY, C, C), V(128, 256), V(4, 128, 256), V(256, 256), V(4, 256, 256),
            V(128, 256), V(1024, 256), V(512, 128),
            V(4, NA, 4, 16, C), V(4, NA, 4, 16, C), V(2, KX, 16, C), V(2, NB, 4, 16, C),
            V(2, NB, 4, 16, C), V(2, NB, 4, 16, C), V(4, NA, 4, 16, C),
            D((4,)), D((2,)), D((5,)), D(()), D((4,)), D(()), D((2,)), D(()), D((2,)), D(()), D((4,)),
        ],
        compiler_params=pltpu.CompilerParams(collective_id=0, has_side_effects=True, vmem_limit_bytes=40 << 20),
        name="spectral",
    )(grid_features, weight_real.reshape(4, KY, C, C), weight_imag.reshape(4, KY, C, C), mode_keep,
      jnp.asarray(t1), jnp.asarray(t2), jnp.asarray(t3), jnp.asarray(t4), jnp.asarray(t5))

    return pl.pallas_call(
        final_kernel,
        grid=(8, 2),
        out_shape=jax.ShapeDtypeStruct((8, 16, NZ, C), BF),
        in_specs=[
            pl.BlockSpec((4, 2, NZ, C), lambda j, x: (x, j, 0, 0)),
            pl.BlockSpec((1, NA, 2, 16, C), lambda j, x: (j // 2, 0, j % 2, 0, 0)),
            pl.BlockSpec((C, C), lambda j, x: (0, 0)),
            pl.BlockSpec((1, C), lambda j, x: (0, 0)),
            pl.BlockSpec((256, 256), lambda j, x: (0, 0)),
        ],
        out_specs=pl.BlockSpec((4, 2, NZ, C), lambda j, x: (x, j, 0, 0)),
        scratch_shapes=[V(8, 256, 256), V(256, 256)],
        compiler_params=pltpu.CompilerParams(vmem_limit_bytes=20 << 20),
        name="combine",
    )(grid_features, back, local_weight, local_bias.reshape(1, C), jnp.asarray(t6))


def solution(mesh):
    in_specs = (P("aa", "ba", None, None), P("ba", None, "aa", None, None), P("ba", None, "aa", None, None),
                P("ba", "aa"), P(), P())
    return jax.shard_map(per_device, mesh=mesh, in_specs=in_specs, out_specs=P("aa", "ba", None, None), check_vma=False)
```

time: 111 us -> 72 us (0.65); the launches traced: 111 us -> 70.6 us
  Pallas kernels: 0 us -> 60.9 us
  waiting for transfers between devices: 42.1 us -> 0 us
  matrix products: 35.7 us -> 0 us
  starting transfers between devices: 16.3 us -> 0 us
  blocking collectives: 9.91 us -> 0 us
  local copies, waits for them, and re-layouts: 5.79 us -> 9.66 us
    pallas_call x0 -> x2, Pallas kernels: none -> 60.9 us  [the longest x1 49.1 us: per_device(): pl.pallas_call(spectral_kernel, out_shape=jax.ShapeDtypeStruct((4, NA, 4,...]
    all_to_all x3 -> x0, waiting for transfers between devices: 42.1 us -> none  [sent_together(): lax.all_to_all(both, axis, split_axis=split_dim, concat_axis=concat_dim,...]
    dot_general x11 -> x0, matrix products: 35.7 us -> none  [the longest x1 12.2 us: per_device(): jnp.einsum('xyzc,cd->xyzd', grid_features, local_weight, preferred_elemen...]
    all_to_all x3 -> x0, starting transfers between devices: 16.3 us -> none  [sent_together(): lax.all_to_all(both, axis, split_axis=split_dim, concat_axis=concat_dim,...]
    all_to_all x1 -> x0, blocking collectives: 9.91 us -> none  [sent_together(): lax.all_to_all(both, axis, split_axis=split_dim, concat_axis=concat_dim,...]
    unnamed x16 -> x23, local copies, waits for them, and re-layouts: 0.31 us -> 9.66 us
    concatenate x4 -> x0, local copies, waits for them, and re-layouts: 3.9 us -> none  [sent_together(): both = jnp.concatenate(arrays, axis=along)]
  transfers between devices with their start and end apart: 3 -> 0, of which waited for: 3 -> 0; matrix products, arithmetic and copies ran while one was open for 0% -> 0% of each run, Pallas kernels for 0% -> 0%
where the time goes in v1:
time: 72 us; the launch traced here: 70.6 us
  Pallas kernels  60.9 us (85%)
  local copies, waits for them, and re-layouts  9.66 us (13%)
    pallas_call x1, Pallas kernels, per_device(): pl.pallas_call(spectral_kernel, out_shape=jax.ShapeDtypeStruct((4, NA, 4,...  49.1 us
    pallas_call x1, Pallas kernels, per_device(): pl.pallas_call(final_kernel, grid=(8, 2), out_shape=jax.ShapeDtypeStruct(...  11.9 us
    unnamed x23, local copies, waits for them, and re-layouts  9.66 us

profile of v1, /device:TPU:0, one launch (start us, length us, event | category | flops | bytes accessed | tf_op | source)
XLA Modules:
  0.0 70.6 jit_solution(9860012843483720802)
XLA Ops:
  0.0 0.7 %copy.13.keep_ref = s32[4,1]{1,0:T(4,128)S(1)} copy(s32[4,1]{0,1:T(1,128)} %param.15) | data formatting | bytes 32 | tf_op args[3]
  0.7 0.0 copy-start.1
  0.7 2.2 %copy-done.1 = bf16[4,32,1,128,128]{4,3,2,1,0:T(8,128)(2,1)S(1)} copy-done((bf16[4,32,1,128,128]{4,3,2,1,0:T(8,128)(2,1)S(1)}, bf16[4,32,1,128,128]{4,3,2,1,0:T(8,128)(2,1)}, u32[]{:S(2)}) %copy-start.1) | copy-done | bytes 4194328
  2.9 0.0 copy-start.2
  2.9 2.2 %copy-done.2 = bf16[4,32,1,128,128]{4,3,2,1,0:T(8,128)(2,1)S(1)} copy-done((bf16[4,32,1,128,128]{4,3,2,1,0:T(8,128)(2,1)S(1)}, bf16[4,32,1,128,128]{4,3,2,1,0:T(8,128)(2,1)}, u32[]{:S(2)}) %copy-start.2) | copy-done | bytes 4194328
  5.1 0.0 copy-start.3
  5.1 1.0 %copy-done.3 = bf16[1024,256]{1,0:T(8,128)(2,1)S(1)} copy-done((bf16[1024,256]{1,0:T(8,128)(2,1)S(1)}, bf16[1024,256]{1,0:T(8,128)(2,1)}, u32[]{:S(2)}) %copy-start.3) | copy-done | bytes 524312
  6.2 0.0 copy-start.4
  6.2 0.9 %copy-done.4 = bf16[512,128]{1,0:T(8,128)(2,1)S(1)} copy-done((bf16[512,128]{1,0:T(8,128)(2,1)S(1)}, bf16[512,128]{1,0:T(8,128)(2,1)}, u32[]{:S(2)}) %copy-start.4) | copy-done | bytes 131096
  7.1 0.0 copy-start.5
  7.1 0.9 %copy-done.5 = bf16[256,256]{1,0:T(8,128)(2,1)S(1)} copy-done((bf16[256,256]{1,0:T(8,128)(2,1)S(1)}, bf16[256,256]{1,0:T(8,128)(2,1)}, u32[]{:S(2)}) %copy-start.5) | copy-done | bytes 131096
  8.0 0.0 copy-start.7
  8.0 0.8 %copy-done.7 = bf16[128,256]{1,0:T(8,128)(2,1)S(1)} copy-done((bf16[128,256]{1,0:T(8,128)(2,1)S(1)}, bf16[128,256]{1,0:T(8,128)(2,1)}, u32[]{:S(2)}) %copy-start.7) | copy-done | bytes 65560
  8.8 0.0 copy-start.8
  8.8 0.8 %copy-done.8 = bf16[128,256]{1,0:T(8,128)(2,1)S(1)} copy-done((bf16[128,256]{1,0:T(8,128)(2,1)S(1)}, bf16[128,256]{1,0:T(8,128)(2,1)}, u32[]{:S(2)}) %copy-start.8) | copy-done | bytes 65560
  9.7 0.0 copy-start
  9.7 0.0 copy-start.6
  9.7 0.0 copy-start.9
  9.7 0.0 copy-start.10
  9.7 49.1 %spectral.1.back_ref = bf16[4,16,4,16,128]{4,3,2,1,0:T(8,128)(2,1)S(1)} custom-call(bf16[8,16,256,128]{3,2,1,0:T(8,128)(2,1)} %x_ref.1, bf16[4,32,128,128]{3,2,1,0:T(8,128)(2,1)S(1)} %bitcast.3, bf16[4,32,128,128]{3,2,1,0:T(8,128)(2,1)S(1)} %bitcast.4, s32[4,1]{1,0:T(4,128)S(1)} %copy.13.keep_ref, bf16[128,256]{1,0:T(8,128)(2,1)S(1)} %copy-done.8, ...), custom_call_target="tpu_custom_call" | custom-call | tf_op jit(solution)/shard_map/spectral/pallas_call | solution.py:224
  58.7 0.0 copy-done
  58.8 0.0 copy-done.6
  58.8 0.0 copy-done.9
  58.8 0.0 copy-done.10
  58.8 11.9 %combine.1 = bf16[8,16,256,128]{3,2,1,0:T(8,128)(2,1)} custom-call(bf16[8,16,256,128]{3,2,1,0:T(8,128)(2,1)S(1)} %copy-done, bf16[4,16,4,16,128]{4,3,2,1,0:T(8,128)(2,1)S(1)} %spectral.1.back_ref, bf16[128,128]{1,0:T(8,128)(2,1)S(1)} %copy-done.9, bf16[1,128]{1,0:T(2,128)(2,1)S(1)} %bitcast.5, bf16[256,256]{1,0:T(8,128)(2,1)S(1)} %copy-done.6), custom_call_target="tpu_custom_call" | custom-call | tf_op jit(solution)/shard_map/combine/pallas_call | solution.py:241
Async XLA Ops:
  0.7 2.2 %copy-start.1 = (bf16[4,32,1,128,128]{4,3,2,1,0:T(8,128)(2,1)S(1)}, bf16[4,32,1,128,128]{4,3,2,1,0:T(8,128)(2,1)}, u32[]{:S(2)}) copy-start(bf16[4,32,1,128,128]{4,3,2,1,0:T(8,128)(2,1)} %param.13) | copy-start | bytes 12582916
  2.9 2.2 %copy-start.2 = (bf16[4,32,1,128,128]{4,3,2,1,0:T(8,128)(2,1)S(1)}, bf16[4,32,1,128,128]{4,3,2,1,0:T(8,128)(2,1)}, u32[]{:S(2)}) copy-start(bf16[4,32,1,128,128]{4,3,2,1,0:T(8,128)(2,1)} %param.14) | copy-start | bytes 12582916
  5.1 1.0 %copy-start.3 = (bf16[1024,256]{1,0:T(8,128)(2,1)S(1)}, bf16[1024,256]{1,0:T(8,128)(2,1)}, u32[]{:S(2)}) copy-start(bf16[1024,256]{1,0:T(8,128)(2,1)} %constant.15.clone.t4_hbm) | copy-start | bytes 1572868
  6.2 0.9 %copy-start.4 = (bf16[512,128]{1,0:T(8,128)(2,1)S(1)}, bf16[512,128]{1,0:T(8,128)(2,1)}, u32[]{:S(2)}) copy-start(bf16[512,128]{1,0:T(8,128)(2,1)} %constant.16.clone.t5_hbm) | copy-start | bytes 393220
  7.1 0.9 %copy-start.5 = (bf16[256,256]{1,0:T(8,128)(2,1)S(1)}, bf16[256,256]{1,0:T(8,128)(2,1)}, u32[]{:S(2)}) copy-start(bf16[256,256]{1,0:T(8,128)(2,1)} %constant.13.clone.t2_hbm) | copy-start | bytes 393220
  8.0 0.8 %copy-start.7 = (bf16[128,256]{1,0:T(8,128)(2,1)S(1)}, bf16[128,256]{1,0:T(8,128)(2,1)}, u32[]{:S(2)}) copy-start(bf16[128,256]{1,0:T(8,128)(2,1)} %constant.14.clone.t3_hbm) | copy-start | bytes 196612
  8.8 0.8 %copy-start.8 = (bf16[128,256]{1,0:T(8,128)(2,1)S(1)}, bf16[128,256]{1,0:T(8,128)(2,1)}, u32[]{:S(2)}) copy-start(bf16[128,256]{1,0:T(8,128)(2,1)} %constant.12.clone.t1_hbm) | copy-start | bytes 196612
  9.7 49.1 %copy-start = (bf16[8,16,256,128]{3,2,1,0:T(8,128)(2,1)S(1)}, bf16[8,16,256,128]{3,2,1,0:T(8,128)(2,1)}, u32[]{:S(2)}) copy-start(bf16[8,16,256,128]{3,2,1,0:T(8,128)(2,1)} %x_ref.1) | copy-start | bytes 25165828
  9.7 49.1 %copy-start.6 = (bf16[256,256]{1,0:T(8,128)(2,1)S(1)}, bf16[256,256]{1,0:T(8,128)(2,1)}, u32[]{:S(2)}) copy-start(bf16[256,256]{1,0:T(8,128)(2,1)} %constant.17.clone.t6_ref) | copy-start | bytes 393220
  9.7 49.1 %copy-start.9 = (bf16[128,128]{1,0:T(8,128)(2,1)S(1)}, bf16[128,128]{1,0:T(8,128)(2,1)}, u32[]{:S(2)}) copy-start(bf16[128,128]{1,0:T(8,128)(2,1)} %w_ref.1) | copy-start | bytes 98308
  9.7 49.1 %copy-start.10 = (bf16[128]{0:T(256)(128)(2,1)S(1)}, bf16[128]{0:T(256)(128)(2,1)}, u32[]{:S(2)}) copy-start(bf16[128]{0:T(256)(128)(2,1)} %param.17) | copy-start | bytes 772

commit v2 on v1

v2 whole, which is shorter than its diff:
```python
import numpy as np
import jax
import jax.numpy as jnp
from jax import lax
from jax.experimental import pallas as pl
from jax.experimental.pallas import tpu as pltpu
from jax.sharding import PartitionSpec as P

NX, NY, NZ, C = 128, 128, 256, 128
KX, KY, KZ = 32, 32, 16
NA, NB = 16, 8
MESH = pl.DeviceIdType.MESH
BF = jnp.bfloat16
F32 = jnp.float32

AA_ORDER = [(2, 2), (3, 2), (1, 2), (2, 3), (2, 1), (3, 1), (1, 3), (3, 3), (1, 1), (0, 2),
            (2, 0), (0, 3), (3, 0), (0, 1), (1, 0)]
BA_ORDER = [(2, 1), (2, 0), (1, 1), (3, 1), (1, 0), (3, 0), (0, 1)]


def kept(length, number):
    j = np.arange(number)
    return np.where(j < number // 2, j, j + length - number)


def angle(k, n, length):
    return 2.0 * np.pi * ((k * n) % length) / length


def complex_block(theta, ri_out, ri_in, sign):
    c, s = np.cos(theta), sign * np.sin(theta)
    return np.where(ri_out == ri_in, c, np.where(ri_out == 0, -s, s))


def tables():
    kx, ky = kept(NX, KX), kept(NY, KY)
    k, _, r, z = np.ix_(np.arange(KZ), np.arange(4), np.arange(2), np.arange(NZ))
    th = angle(k, z, NZ)
    t1 = np.where(r == 0, np.cos(th), -np.sin(th)) + np.zeros((KZ, 4, 2, NZ))
    t1 = t1.reshape(128, 256)
    k, _, r, x, q = np.ix_(kx, np.arange(2), np.arange(2), np.arange(NX), np.arange(2))
    t2 = complex_block(angle(k, x, NX), r, q, -1) + np.zeros((KX, 2, 2, NX, 2))
    t2 = t2.reshape(128, 256)
    k8, m, k4, r, g, b, yh, n, yl, q = np.ix_(*map(np.arange, (8, 2, 4, 2, 4, NB, 2, 2, 2, 2)))
    th = angle(ky[k8 * 4 + k4], b * 16 + g * 4 + yh * 2 + yl, NY)
    f = (complex_block(th, r, q, -1) * (m == n)).reshape(8, 2, 4, 2, 512)
    t3 = np.stack([f, np.stack([-f[:, :, :, 1], f[:, :, :, 0]], axis=3)]).reshape(256, 512)
    g, b, y, m, r, p, k8, n, k4, q = np.ix_(*map(np.arange, (4, NB, 4, 4, 2, 2, 8, 2, 4, 2)))
    t4 = complex_block(angle(ky[k8 * 4 + k4], b * 16 + g * 4 + y, NY), r, q, 1) * (m == 2 * p + n)
    t4 = t4.reshape(1024, 256)
    y, x, r, b, w, m, q = np.ix_(np.arange(2), np.arange(NX), np.arange(2), np.arange(NB), np.arange(2),
                                 np.arange(4), np.arange(2))
    t5 = complex_block(angle(kx[b * 4 + m], x, NX), r, q, 1) * (y == w)
    t5 = t5.reshape(512, 128)
    z, k, _, r = np.ix_(np.arange(NZ), np.arange(KZ), np.arange(8), np.arange(2))
    th = angle(k, z, NZ)
    t6 = np.where(r == 0, np.cos(th), -np.sin(th)) * np.where(k == 0, 1.0, 2.0) / (NX * NY * NZ) * 0.5
    t6 = (t6 + np.zeros((NZ, KZ, 8, 2))).reshape(256, 256)
    return [np.asarray(t, np.float32).astype(jnp.bfloat16) for t in (t1, t2, t3, t4, t5, t6)]


def dot(a, b):
    return jnp.dot(a, b, preferred_element_type=F32)


def bias_row(bias_ref):
    bias = bias_ref[...].astype(F32) * 0.5
    return jnp.concatenate([bias, bias], axis=1)


def back_pair(back_ref, y):
    return jnp.concatenate([back_ref[:, y].reshape(256, C), back_ref[:, y + 1].reshape(256, C)], axis=1)


def combine(first, second, weights, inverse, back, bias):
    c0 = np.float32(2.0 * np.sqrt(2.0 / np.pi))
    c1 = np.float32(8.0 * 0.044715 * np.sqrt(2.0 / np.pi))
    v = dot(jnp.concatenate([first, second], axis=1), weights) + dot(inverse, back) + bias
    return (v + v * jnp.tanh(v * (c0 + c1 * (v * v)))).astype(BF)


def spectral_kernel(x_hbm, wr_hbm, wi_hbm, keep_hbm, t1_hbm, t2_hbm, t3_hbm, t4_hbm, t5_hbm, t6_hbm, w_hbm, bias_hbm,
                    out_ref, xlast, blast, t6m, wbd,
                    xv, wv, keep_ref, t1v, t1m, t2v, t2m, t3v, t4v, t5v, t6v, lw, bias_ref, s1, r1, s2, r2, s3, r3, s4, r4,
                    xsem, wsem, tsem, sa, ra, sb, rb, sc, rc, sd, rd):
    ia, ib = lax.axis_index("aa"), lax.axis_index("ba")
    ix, iz, iy, ic = ia // 4, lax.rem(ia, 4), ib // 2, lax.rem(ib, 2)
    aa_peers = [lax.rem(ix + dx, 4) * 4 + lax.rem(iz + dz, 4) for dx, dz in AA_ORDER]
    ba_peers = [lax.rem(iy + dy, 4) * 2 + lax.rem(ic + dc, 2) for dy, dc in BA_ORDER]

    tcopies = [pltpu.make_async_copy(src, dst, tsem.at[i]) for i, (src, dst) in enumerate(
        [(t1_hbm, t1v), (t2_hbm, t2v), (t3_hbm, t3v), (t4_hbm, t4v), (t5_hbm, t5v), (t6_hbm, t6v), (w_hbm, lw), (bias_hbm, bias_ref)])]
    tcopies[0].start()
    xg = [xv.at[0], xv.at[1], xv.at[2], xlast]
    xcopies = [pltpu.make_async_copy(x_hbm.at[:, pl.ds(4 * g, 4)], xg[g], xsem.at[g]) for g in range(4)]
    for c in xcopies:
        c.start()
    tcopies[1].start()
    wcopies = [pltpu.make_async_copy(wr_hbm, wv.at[0], wsem.at[0]), pltpu.make_async_copy(wi_hbm, wv.at[1], wsem.at[1]),
               pltpu.make_async_copy(keep_hbm, keep_ref, wsem.at[2])]

    barrier = pltpu.get_barrier_semaphore()
    for t in aa_peers:
        pl.semaphore_signal(barrier, inc=1, device_id={"aa": t}, device_id_type=MESH)
    for t in ba_peers:
        pl.semaphore_signal(barrier, inc=1, device_id={"ba": t}, device_id_type=MESH)

    def send_aa(src, dst, ssem, rsem):
        for t in aa_peers:
            pltpu.make_async_remote_copy(src.at[t], dst.at[ia], ssem, rsem, device_id={"aa": t}, device_id_type=MESH).start()

    def send_ba(src, dst, ssem, rsem):
        for t in ba_peers:
            pltpu.make_async_remote_copy(src(t), dst.at[ib], ssem, rsem, device_id={"ba": t}, device_id_type=MESH).start()

    def wait_bytes(ref, sem):
        pltpu.make_async_copy(ref, ref, sem).wait()

    tcopies[0].wait()
    rows1 = lax.broadcasted_iota(jnp.int32, (128, 256), 0) // 2 % 4
    for i in range(4):
        t1m[i] = jnp.where(rows1 == i, t1v[...].astype(F32), 0.0).astype(BF)
    for g in range(4):
        xcopies[g].wait()
        for y in range(4):
            acc = None
            for i in range(4):
                rhs = jnp.concatenate([xg[g][i, y], xg[g][i + 4, y]], axis=1)
                p = dot(t1m[i], rhs)
                acc = p if acc is None else acc + p
            acc = acc.reshape(KZ, 8, 256)
            s1[g, :, y] = jnp.concatenate([acc[:, :, :128], acc[:, :, 128:]], axis=1).astype(BF)
        if g == 0:
            pl.semaphore_wait(barrier, len(aa_peers) + len(ba_peers))
        send_aa(s1.at[g], r1.at[g], sa, ra.at[g])
        r1[g, ia] = s1[g, ia]

    for c in tcopies[2:] + wcopies:
        c.start()
    tcopies[1].wait()
    rows2 = lax.broadcasted_iota(jnp.int32, (128, 256), 0) // 2 % 2
    for i in range(2):
        t2m[i] = jnp.where(rows2 == i, t2v[...].astype(F32), 0.0).astype(BF)
    for c in tcopies[2:]:
        c.wait()
    lanes6 = lax.broadcasted_iota(jnp.int32, (256, 256), 1) // 2 % 8
    for i in range(8):
        t6m[i] = jnp.where(lanes6 == i, t6v[...].astype(F32), 0.0).astype(BF)
    half_w = (lw[...].astype(F32) * 0.5).astype(BF)
    zero_w = jnp.zeros_like(half_w)
    wbd[...] = jnp.concatenate([jnp.concatenate([half_w, zero_w], axis=1), jnp.concatenate([zero_w, half_w], axis=1)], axis=0)

    for g in range(4):
        wait_bytes(r1.at[g, pl.ds(0, NA - 1)], ra.at[g])
        acc = None
        for i in range(2):
            rhs = jnp.concatenate([r1[g, :, i].reshape(256, C), r1[g, :, i + 2].reshape(256, C)], axis=1)
            p = dot(t2m[i], rhs)
            acc = p if acc is None else acc + p
        acc = acc.reshape(KX // 2, 8, 256)
        s2[g] = jnp.concatenate([acc[:, :, :C], acc[:, :, C:]], axis=1).astype(BF)
        send_ba(lambda t: s2.at[g, pl.ds(2 * t, 2)], r2.at[g], sb, rb.at[g])
        r2[g, ib] = s2[g, pl.ds(2 * ib, 2)]

    for c in wcopies:
        c.wait()
    for g in range(4):
        wait_bytes(r2.at[g, pl.ds(0, NB - 1)], rb.at[g])

    block = lax.broadcasted_iota(jnp.int32, (16, 256), 0) // 2 % 4
    row = lax.broadcasted_iota(jnp.int32, (16, C), 0)
    mixed = []
    for p in range(2):
        spec = dot(t3v[...], r2[:, :, p].reshape(512, C))
        keep = jnp.where(row < 8, keep_ref[0, 2 * p], keep_ref[0, 2 * p + 1])
        for q in range(8):
            lhs = jnp.concatenate([spec[16 * q:16 * q + 16], spec[128 + 16 * q:128 + 16 * q + 16]], axis=1)
            acc = None
            for j in range(4):
                k = 4 * q + j
                w = jnp.concatenate([jnp.concatenate([wv[r, 2 * p, k], wv[r, 2 * p + 1, k]], axis=1) for r in range(2)], axis=0)
                part = dot(jnp.where(block == j, lhs, 0.0).astype(BF), w)
                acc = part if acc is None else acc + part
            position = 4 * q + row // 2 % 4
            level = jnp.where(position < KY // 2, position, KY - 1 - position)
            mixed.append(jnp.where(level < keep, jnp.where(row < 8, acc[:, :C], acc[:, C:]), 0.0))
    rhs = jnp.concatenate(mixed, axis=0).astype(BF)
    for g in range(4):
        s3[g] = dot(t4v[pl.ds(256 * g, 256)], rhs).astype(BF).reshape(NB, 2, 16, C)
        send_ba(lambda t: s3.at[g, t], r3.at[g], sc, rc.at[g])
        r3[g, ib] = s3[g, ib]

    for g in range(4):
        wait_bytes(r3.at[g, pl.ds(0, NB - 1)], rc.at[g])
        rhs = jnp.concatenate([r3[g, :, 0].reshape(128, C), r3[g, :, 1].reshape(128, C)], axis=1)
        for i in range(2):
            back = dot(t5v[pl.ds(256 * i, 256)], rhs).astype(BF)
            for half in range(2):
                s4[g, :, 2 * half + i] = back[:, C * half:C * half + C].reshape(NA, 16, C)
        land = r4.at[g] if g < 3 else blast
        send_aa(s4.at[g], land, sd, rd.at[g])
        land[ia] = s4[g, ia]

    bias = bias_row(bias_ref)
    for g in range(3):
        wait_bytes(r4.at[g, pl.ds(0, NA - 1)], rd.at[g])
        for y in (0, 2):
            rhs = back_pair(r4.at[g], y)
            for x in range(8):
                o = combine(xv[g, x, y], xv[g, x, y + 1], wbd[...], t6m[x], rhs, bias)
                out_ref[x, 4 * g + y] = o[:, :C]
                out_ref[x, 4 * g + y + 1] = o[:, C:]

    wait_bytes(blast.at[pl.ds(0, NA - 1)], rd.at[3])
    wait_bytes(s1.at[:, pl.ds(0, NA - 1)], sa)
    wait_bytes(s4.at[:, pl.ds(0, NA - 1)], sd)
    wait_bytes(r2.at[:, pl.ds(0, NB - 1)], sb)
    wait_bytes(r3.at[:, pl.ds(0, NB - 1)], sc)


def store_kernel(val_ref, xlast, blast, t6m, wbd, bias_ref, out_ref, tail, sem):
    copies = [pltpu.make_async_copy(val_ref.at[i], out_ref.at[i, pl.ds(0, 12)], sem.at[i]) for i in range(8)]
    tails = [pltpu.make_async_copy(tail.at[i], out_ref.at[i, pl.ds(12, 4)], sem.at[8 + i]) for i in range(8)]
    for c in copies:
        c.start()
    bias = bias_row(bias_ref)
    rhs = [back_pair(blast, y) for y in (0, 2)]
    for x in range(8):
        for i in range(2):
            o = combine(xlast[x, 2 * i], xlast[x, 2 * i + 1], wbd[...], t6m[x], rhs[i], bias)
            tail[x, 2 * i] = o[:, :C]
            tail[x, 2 * i + 1] = o[:, C:]
        if x > 0:
            tails[x - 1].start()
    tails[7].start()
    for c in copies + tails:
        c.wait()


def per_device(grid_features, weight_real, weight_imag, mode_keep, local_weight, local_bias):
    t1, t2, t3, t4, t5, t6 = tables()
    any_spec = pl.BlockSpec(memory_space=pltpu.HBM)
    vmem_spec = pl.BlockSpec(memory_space=pltpu.VMEM)
    V = lambda *s: pltpu.VMEM(s, BF)
    D = pltpu.SemaphoreType.DMA
    hbm = lambda a: pltpu.with_memory_space_constraint(a, pltpu.HBM)
    results = pl.pallas_call(
        spectral_kernel,
        out_shape=[jax.ShapeDtypeStruct(shape, BF) for shape in (
            (8, 12, NZ, C), (8, 4, NZ, C), (NA, 4, 16, C), (8, 256, 256), (256, 256))],
        in_specs=[any_spec] * 12,
        out_specs=[vmem_spec] * 5,
        scratch_shapes=[
            V(3, 8, 4, NZ, C), V(2, 4, KY, C, C), pltpu.SMEM((1, 4), jnp.int32), V(128, 256), V(4, 128, 256),
            V(128, 256), V(2, 128, 256), V(256, 512), V(1024, 256), V(512, 128), V(256, 256), V(C, C), V(1, C),
            V(4, NA, 4, 16, C), V(4, NA, 4, 16, C), V(4, KX // 2, 16, C), V(4, NB, 2, 16, C),
            V(4, NB, 2, 16, C), V(4, NB, 2, 16, C), V(4, NA, 4, 16, C), V(3, NA, 4, 16, C),
            D((4,)), D((3,)), D((8,)), D(()), D((4,)), D(()), D((4,)), D(()), D((4,)), D(()), D((4,)),
        ],
        compiler_params=pltpu.CompilerParams(collective_id=0, has_side_effects=True, vmem_limit_bytes=40 << 20),
        name="spectral",
    )(*map(hbm, (grid_features, weight_real.reshape(4, KY, C, C), weight_imag.reshape(4, KY, C, C), mode_keep.reshape(1, 4),
                 *map(jnp.asarray, (t1, t2, t3, t4, t5, t6)), local_weight, local_bias.reshape(1, C))))

    return pl.pallas_call(
        store_kernel,
        out_shape=jax.ShapeDtypeStruct((8, 16, NZ, C), BF),
        in_specs=[vmem_spec] * 6,
        out_specs=any_spec,
        scratch_shapes=[V(8, 4, NZ, C), D((16,))],
        compiler_params=pltpu.CompilerParams(vmem_limit_bytes=6 << 20),
        name="store",
    )(*results, local_bias.reshape(1, C))


def solution(mesh):
    in_specs = (P("aa", "ba", None, None), P("ba", None, "aa", None, None), P("ba", None, "aa", None, None),
                P("ba", "aa"), P(), P())
    return jax.shard_map(per_device, mesh=mesh, in_specs=in_specs, out_specs=P("aa", "ba", None, None), check_vma=False)
```

time: 72 us -> 49 us (0.68); the launches traced: 70.6 us -> 48.9 us
  Pallas kernels: 60.9 us -> 48.9 us
  local copies, waits for them, and re-layouts: 9.66 us -> 0.01 us
    pallas_call x2, Pallas kernels: 60.9 us -> 48.9 us  [the longest x1 45.4 us: per_device(): pl.pallas_call(spectral_kernel, out_shape=[jax.ShapeDtypeStruct(shape, BF...]
    unnamed x23 -> x2, local copies, waits for them, and re-layouts: 9.66 us -> 0.01 us
where the time goes in v2:
time: 49 us; the launch traced here: 48.9 us
  Pallas kernels  48.9 us (100%)
    pallas_call x1, Pallas kernels, per_device(): pl.pallas_call(spectral_kernel, out_shape=[jax.ShapeDtypeStruct(shape, BF...  45.4 us
    pallas_call x1, Pallas kernels, per_device(): pl.pallas_call(store_kernel, out_shape=jax.ShapeDtypeStruct((8, 16, NZ, C...  3.42 us

profile of v2, /device:TPU:0, one launch (start us, length us, event | category | flops | bytes accessed | tf_op | source)
XLA Modules:
  0.0 48.9 jit_solution(18046157328242887144)
XLA Ops:
  0.0 0.0 copy-start
  0.0 45.4 %spectral.1 = (bf16[8,12,256,128]{3,2,1,0:T(8,128)(2,1)S(1)}, bf16[8,4,256,128]{3,2,1,0:T(8,128)(2,1)S(1)}, bf16[16,4,16,128]{3,2,1,0:T(8,128)(2,1)S(1)}, bf16[8...) custom-call(bf16[8,16,256,128]{3,2,1,0:T(8,128)(2,1)} %x_hbm.1, bf16[4,32,128,128]{3,2,1,0:T(8,128)(2,1)} %bitcast.6, ...), custom_call_target="tpu_custom_call" | custom-call | tf_op jit(solution)/shard_map/spectral/pallas_call | solution.py:247
  45.4 0.0 copy-done
  45.5 3.4 %store.1 = bf16[8,16,256,128]{3,2,1,0:T(8,128)(2,1)} custom-call(bf16[8,12,256,128]{3,2,1,0:T(8,128)(2,1)S(1)} %get-tuple-element.10.val_ref, bf16[8,4,256,128]{3,2,1,0:T(8,128)(2,1)S(1)} %get-tuple-element.11.xlast, bf16[16,4,16,128]{3,2,1,0:T(8,128)(2,1)S(1)} %get-tuple-element.12.blast, bf16[8,256,256]{2,1,0:T(8,128)(2,1)S(1)} %get-tuple-element.13.t6m, ...), custom_call_target="tpu_custom_call" | custom-call | tf_op jit(solution)/shard_map/store/pallas_call | solution.py:265
Async XLA Ops:
  0.0 45.4 %copy-start = (bf16[128]{0:T(256)(128)(2,1)S(1)}, bf16[128]{0:T(256)(128)(2,1)}, u32[]{:S(2)}) copy-start(bf16[128]{0:T(256)(128)(2,1)} %param.17) | copy-start | bytes 772

commit v3 on v2

--- a/solution.py
+++ b/solution.py
@@ -15,6 +15,7 @@
 
 AA_ORDER = [(2, 2), (3, 2), (1, 2), (2, 3), (2, 1), (3, 1), (1, 3), (3, 3), (1, 1), (0, 2),
             (2, 0), (0, 3), (3, 0), (0, 1), (1, 0)]
+EARLY_FIRST = [0, 1, 3, 4, 12, 2, 5, 7, 8, 13, 15, 6, 9, 11, 14, 10]
 BA_ORDER = [(2, 1), (2, 0), (1, 1), (3, 1), (1, 0), (3, 0), (0, 1)]
 
 
@@ -198,7 +199,13 @@
             for half in range(2):
                 s4[g, :, 2 * half + i] = back[:, C * half:C * half + C].reshape(NA, 16, C)
         land = r4.at[g] if g < 3 else blast
-        send_aa(s4.at[g], land, sd, rd.at[g])
+        if g == 3:
+            for t in EARLY_FIRST:
+                @pl.when(ia != t)
+                def _():
+                    pltpu.make_async_remote_copy(s4.at[g, t], land.at[ia], sd, rd.at[g], device_id={"aa": t}, device_id_type=MESH).start()
+        else:
+            send_aa(s4.at[g], land, sd, rd.at[g])
         land[ia] = s4[g, ia]
 
     bias = bias_row(bias_ref)

time: 49 us -> 48.6 us (level)
  no operation moved by 1% of the time
where the time goes in v3:
time: 48.6 us; the launch traced here: 48.5 us
  Pallas kernels  48.5 us (100%)
    pallas_call x1, Pallas kernels, per_device(): pl.pallas_call(spectral_kernel, out_shape=[jax.ShapeDtypeStruct(shape, BF...  45.1 us
    pallas_call x1, Pallas kernels, per_device(): pl.pallas_call(store_kernel, out_shape=jax.ShapeDtypeStruct((8, 16, NZ, C...  3.42 us

profile of v3, /device:TPU:0, one launch (start us, length us, event | category | flops | bytes accessed | tf_op | source)
XLA Modules:
  0.0 48.5 jit_solution(18127039916724022915)
XLA Ops:
  0.0 0.0 copy-start
  0.0 45.1 %spectral.1 = (bf16[8,12,256,128]{3,2,1,0:T(8,128)(2,1)S(1)}, bf16[8,4,256,128]{3,2,1,0:T(8,128)(2,1)S(1)}, bf16[16,4,16,128]{3,2,1,0:T(8,128)(2,1)S(1)}, bf16[8...) custom-call(bf16[8,16,256,128]{3,2,1,0:T(8,128)(2,1)} %x_hbm.1, bf16[4,32,128,128]{3,2,1,0:T(8,128)(2,1)} %bitcast.6, ...), custom_call_target="tpu_custom_call" | custom-call | tf_op jit(solution)/shard_map/spectral/pallas_call | solution.py:254
  45.1 0.0 copy-done
  45.1 3.4 %store.1 = bf16[8,16,256,128]{3,2,1,0:T(8,128)(2,1)} custom-call(bf16[8,12,256,128]{3,2,1,0:T(8,128)(2,1)S(1)} %get-tuple-element.10.val_ref, bf16[8,4,256,128]{3,2,1,0:T(8,128)(2,1)S(1)} %get-tuple-element.11.xlast, bf16[16,4,16,128]{3,2,1,0:T(8,128)(2,1)S(1)} %get-tuple-element.12.blast, bf16[8,256,256]{2,1,0:T(8,128)(2,1)S(1)} %get-tuple-element.13.t6m, ...), custom_call_target="tpu_custom_call" | custom-call | tf_op jit(solution)/shard_map/store/pallas_call | solution.py:272
Async XLA Ops:
  0.0 45.1 %copy-start = (bf16[128]{0:T(256)(128)(2,1)S(1)}, bf16[128]{0:T(256)(128)(2,1)}, u32[]{:S(2)}) copy-start(bf16[128]{0:T(256)(128)(2,1)} %param.17) | copy-start | bytes 772

commit v4 on v3

--- a/solution.py
+++ b/solution.py
@@ -46,8 +46,8 @@
     th = angle(ky[k8 * 4 + k4], b * 16 + g * 4 + yh * 2 + yl, NY)
     f = (complex_block(th, r, q, -1) * (m == n)).reshape(8, 2, 4, 2, 512)
     t3 = np.stack([f, np.stack([-f[:, :, :, 1], f[:, :, :, 0]], axis=3)]).reshape(256, 512)
-    g, b, y, m, r, p, k8, n, k4, q = np.ix_(*map(np.arange, (4, NB, 4, 4, 2, 2, 8, 2, 4, 2)))
-    t4 = complex_block(angle(ky[k8 * 4 + k4], b * 16 + g * 4 + y, NY), r, q, 1) * (m == 2 * p + n)
+    g, b, y, m, r, p, k8, n, k4, q = np.ix_(*map(np.arange, (8, NB, 2, 4, 2, 2, 8, 2, 4, 2)))
+    t4 = complex_block(angle(ky[k8 * 4 + k4], b * 16 + g * 2 + y, NY), r, q, 1) * (m == 2 * p + n)
     t4 = t4.reshape(1024, 256)
     y, x, r, b, w, m, q = np.ix_(np.arange(2), np.arange(NX), np.arange(2), np.arange(NB), np.arange(2),
                                  np.arange(4), np.arange(2))
@@ -165,14 +165,16 @@
 
     for c in wcopies:
         c.wait()
-    for g in range(4):
+    for g in range(3):
         wait_bytes(r2.at[g, pl.ds(0, NB - 1)], rb.at[g])
+    partial = [dot(t3v[:, :384], r2[:3, :, p].reshape(384, C)) for p in range(2)]
+    wait_bytes(r2.at[3, pl.ds(0, NB - 1)], rb.at[3])
 
     block = lax.broadcasted_iota(jnp.int32, (16, 256), 0) // 2 % 4
     row = lax.broadcasted_iota(jnp.int32, (16, C), 0)
     mixed = []
     for p in range(2):
-        spec = dot(t3v[...], r2[:, :, p].reshape(512, C))
+        spec = partial[p] + dot(t3v[:, 384:], r2[3, :, p].reshape(128, C))
         keep = jnp.where(row < 8, keep_ref[0, 2 * p], keep_ref[0, 2 * p + 1])
         for q in range(8):
             lhs = jnp.concatenate([spec[16 * q:16 * q + 16], spec[128 + 16 * q:128 + 16 * q + 16]], axis=1)
@@ -186,25 +188,29 @@
             level = jnp.where(position < KY // 2, position, KY - 1 - position)
             mixed.append(jnp.where(level < keep, jnp.where(row < 8, acc[:, :C], acc[:, C:]), 0.0))
     rhs = jnp.concatenate(mixed, axis=0).astype(BF)
+    for n in range(4):
+        part = dot(t4v[pl.ds(256 * n, 256)], rhs).astype(BF).reshape(2, NB, 16, C)
+        for h in (2 * n, 2 * n + 1):
+            s3[h] = part[h - 2 * n]
+            send_ba(lambda t: s3.at[h, t], r3.at[h], sc, rc.at[h])
+            r3[h, ib] = s3[h, ib]
+
     for g in range(4):
-        s3[g] = dot(t4v[pl.ds(256 * g, 256)], rhs).astype(BF).reshape(NB, 2, 16, C)
-        send_ba(lambda t: s3.at[g, t], r3.at[g], sc, rc.at[g])
-        r3[g, ib] = s3[g, ib]
-
-    for g in range(4):
-        wait_bytes(r3.at[g, pl.ds(0, NB - 1)], rc.at[g])
-        rhs = jnp.concatenate([r3[g, :, 0].reshape(128, C), r3[g, :, 1].reshape(128, C)], axis=1)
-        for i in range(2):
-            back = dot(t5v[pl.ds(256 * i, 256)], rhs).astype(BF)
-            for half in range(2):
-                s4[g, :, 2 * half + i] = back[:, C * half:C * half + C].reshape(NA, 16, C)
+        for n in range(2):
+            wait_bytes(r3.at[2 * g + n, pl.ds(0, NB - 1)], rc.at[2 * g + n])
+            rhs = r3[2 * g + n].reshape(128, C)
+            for i in range(2):
+                s4[g, :, 2 * n + i] = dot(t5v[pl.ds(256 * i, 256)], rhs).astype(BF).reshape(NA, 16, C)
+            if g == 0:
+                for t in aa_peers:
+                    pltpu.make_async_remote_copy(s4.at[g, t, pl.ds(2 * n, 2)], r4.at[g, ia, pl.ds(2 * n, 2)], sd, rd.at[g], device_id={"aa": t}, device_id_type=MESH).start()
         land = r4.at[g] if g < 3 else blast
         if g == 3:
             for t in EARLY_FIRST:
                 @pl.when(ia != t)
                 def _():
                     pltpu.make_async_remote_copy(s4.at[g, t], land.at[ia], sd, rd.at[g], device_id={"aa": t}, device_id_type=MESH).start()
-        else:
+        elif g > 0:
             send_aa(s4.at[g], land, sd, rd.at[g])
         land[ia] = s4[g, ia]
 
@@ -261,8 +267,8 @@
             V(3, 8, 4, NZ, C), V(2, 4, KY, C, C), pltpu.SMEM((1, 4), jnp.int32), V(128, 256), V(4, 128, 256),
             V(128, 256), V(2, 128, 256), V(256, 512), V(1024, 256), V(512, 128), V(256, 256), V(C, C), V(1, C),
             V(4, NA, 4, 16, C), V(4, NA, 4, 16, C), V(4, KX // 2, 16, C), V(4, NB, 2, 16, C),
-            V(4, NB, 2, 16, C), V(4, NB, 2, 16, C), V(4, NA, 4, 16, C), V(3, NA, 4, 16, C),
-            D((4,)), D((3,)), D((8,)), D(()), D((4,)), D(()), D((4,)), D(()), D((4,)), D(()), D((4,)),
+            V(8, NB, 16, C), V(8, NB, 16, C), V(4, NA, 4, 16, C), V(3, NA, 4, 16, C),
+            D((4,)), D((3,)), D((8,)), D(()), D((4,)), D(()), D((4,)), D(()), D((8,)), D(()), D((4,)),
         ],
         compiler_params=pltpu.CompilerParams(collective_id=0, has_side_effects=True, vmem_limit_bytes=40 << 20),
         name="spectral",

time: 48.6 us -> 49 us (level)
  no operation moved by 1% of the time
where the time goes in v4:
time: 49 us; the launch traced here: 48.9 us
  Pallas kernels  48.9 us (100%)
    pallas_call x1, Pallas kernels, per_device(): pl.pallas_call(spectral_kernel, out_shape=[jax.ShapeDtypeStruct(shape, BF...  45.5 us
    pallas_call x1, Pallas kernels, per_device(): pl.pallas_call(store_kernel, out_shape=jax.ShapeDtypeStruct((8, 16, NZ, C...  3.42 us

profile of v4, /device:TPU:0, one launch (start us, length us, event | category | flops | bytes accessed | tf_op | source)
XLA Modules:
  0.0 48.9 jit_solution(2122194514796972161)
XLA Ops:
  0.0 0.0 copy-start
  0.0 45.5 %spectral.1 = (bf16[8,12,256,128]{3,2,1,0:T(8,128)(2,1)S(1)}, bf16[8,4,256,128]{3,2,1,0:T(8,128)(2,1)S(1)}, bf16[16,4,16,128]{3,2,1,0:T(8,128)(2,1)S(1)}, bf16[8...) custom-call(bf16[8,16,256,128]{3,2,1,0:T(8,128)(2,1)} %x_hbm.1, bf16[4,32,128,128]{3,2,1,0:T(8,128)(2,1)} %bitcast.6, ...), custom_call_target="tpu_custom_call" | custom-call | tf_op jit(solution)/shard_map/spectral/pallas_call | solution.py:260
  45.5 0.0 copy-done
  45.5 3.4 %store.1 = bf16[8,16,256,128]{3,2,1,0:T(8,128)(2,1)} custom-call(bf16[8,12,256,128]{3,2,1,0:T(8,128)(2,1)S(1)} %get-tuple-element.10.val_ref, bf16[8,4,256,128]{3,2,1,0:T(8,128)(2,1)S(1)} %get-tuple-element.11.xlast, bf16[16,4,16,128]{3,2,1,0:T(8,128)(2,1)S(1)} %get-tuple-element.12.blast, bf16[8,256,256]{2,1,0:T(8,128)(2,1)S(1)} %get-tuple-element.13.t6m, ...), custom_call_target="tpu_custom_call" | custom-call | tf_op jit(solution)/shard_map/store/pallas_call | solution.py:278
Async XLA Ops:
  0.0 45.5 %copy-start = (bf16[128]{0:T(256)(128)(2,1)S(1)}, bf16[128]{0:T(256)(128)(2,1)}, u32[]{:S(2)}) copy-start(bf16[128]{0:T(256)(128)(2,1)} %param.17) | copy-start | bytes 772
